TPU v7x, 32 devices: a whole 2x2x4 slice. The times are simulated.
32 devices in a mesh: rows: 8 (over y, x, core), sub: 4 (over z).
Axes of the slice: x: 2, y: 2, z: 4, core: 2. Of those that a mesh axis runs over, the one named last changes fastest.
Arguments:
- u_fem: float32 [120, 524288], P(None, ('rows', 'sub')), may hold values from -600 to 600
- resid_fem: float32 [1, 524288], P(None, ('rows', 'sub')), may hold values from -60 to 60
- slot_map: int32 [32, 32], P(('rows', 'sub')), may hold values from 0 to 31, as said below
- restart: float32 [120, 40], replicated, may hold values from -0.5 to 0.5
- coeff: float32 [3, 120, 120], P(None, None, 'sub'), may hold values from -6 to 6
Outputs:
- new_basis: float32 [40, 524288], P(None, ('rows', 'sub'))
- next_vector: float32 [1, 524288], P(None, ('rows', 'sub'))
- new_coeff: float32 [3, 40, 120], replicated
Inputs may be any that keep to these rules, and one draw needn't show every extreme that they name: Each row of slot_map is a permutation of 0 to 31.
All inputs are finite; a program needn't handle non-finite values.
Results may differ from a plain program's by a relative error of at most 0.00015.
Values sent between devices are 32-bit elements; how exact they have to be, the bound alone decides.
A program may use at most 64 MiB of HBM per device.

v0:
```python
import functools

import jax
import jax.numpy as jnp
from jax import lax
from jax.experimental import pallas as pl
from jax.experimental.pallas import tpu as pltpu

HIGHEST = lax.Precision.HIGHEST
MESH = pl.DeviceIdType.MESH
AXES = ("rows", "sub")
LANES = 128


def me_of(ns):
    return lax.axis_index("rows") * ns + lax.axis_index("sub")


def greet_all(me, ndev, ns):
    barrier = pltpu.get_barrier_semaphore()

    def greet(o, carry):
        j = (me + o) % ndev
        pl.semaphore_signal(barrier, inc=1, device_id=(j // ns, j % ns), device_id_type=MESH)
        return carry

    lax.fori_loop(1, ndev, greet, 0)
    return barrier


def gram_kernel(ndev, ns, chunk, u_hbm, r_hbm, out_ref, u_ref, r_ref, stage, rs_buf, red, ag_buf,
                in_sem, s1, r1, s2, r2):
    me = me_of(ns)
    pieces = u_ref.shape[1] // chunk
    load_r = pltpu.make_async_copy(r_hbm, r_ref, in_sem.at[pieces])
    load_r.start()
    loads = []
    for c in range(pieces):
        cols = pl.ds(c * chunk, chunk)
        loads.append(pltpu.make_async_copy(u_hbm.at[:, cols], u_ref.at[:, cols], in_sem.at[c]))
        loads[-1].start()
    barrier = greet_all(me, ndev, ns)
    width = out_ref.shape[1]
    pad = width - u_ref.shape[0]
    rpd = width // ndev

    def piece(c, acc):
        loads[c].wait()
        cols = pl.ds(c * chunk, chunk)
        first = lax.broadcasted_iota(jnp.int32, (pad, chunk), 0) == 0
        tail = jnp.where(first, jnp.broadcast_to(r_ref[:, cols], (pad, chunk)), 0.0)
        x = jnp.concatenate([u_ref[:, cols], tail], axis=0)
        hi = x.astype(jnp.bfloat16)
        lo = (x - hi.astype(jnp.float32)).astype(jnp.bfloat16)
        both = jnp.concatenate([hi, lo], axis=0)
        return acc + lax.dot_general(both, both, (((1,), (1,)), ((), ())), preferred_element_type=jnp.float32)

    load_r.wait()
    full = jnp.zeros((2 * width, 2 * width), jnp.float32)
    for c in range(pieces):
        full = piece(c, full)
    cross = full[:width, width:]
    gram = full[:width, :width] + (cross + cross.T) + full[width:, width:]
    for i in range(ndev):
        stage[i] = gram[i * rpd : (i + 1) * rpd, :]
    rs_buf[me] = stage[me]
    pl.semaphore_wait(barrier, ndev - 1)

    def scatter_copy(j, slot):
        return pltpu.make_async_remote_copy(
            src_ref=stage.at[j], dst_ref=rs_buf.at[slot], send_sem=s1.at[j], recv_sem=r1.at[slot],
            device_id=(j // ns, j % ns), device_id_type=MESH)

    def gather_copy(j, slot):
        return pltpu.make_async_remote_copy(
            src_ref=red, dst_ref=ag_buf.at[slot], send_sem=s2.at[j], recv_sem=r2.at[slot],
            device_id=(j // ns, j % ns), device_id_type=MESH)

    def loop(action):
        def body(o, carry):
            action((me + o) % ndev)
            return carry
        lax.fori_loop(1, ndev, body, 0)

    loop(lambda j: scatter_copy(j, me).start())
    loop(lambda j: scatter_copy(j, j).wait_recv())
    total = jnp.sum(rs_buf[...], axis=0)
    red[...] = total
    ag_buf[me] = total
    loop(lambda j: gather_copy(j, me).start())
    loop(lambda j: gather_copy(j, j).wait_recv())
    for i in range(ndev):
        out_ref[i * rpd : (i + 1) * rpd, :] = ag_buf[i]
    loop(lambda j: scatter_copy(j, me).wait_send())
    loop(lambda j: gather_copy(j, me).wait_send())


def gram_sums(u, r, ndev, ns):
    width = LANES
    rpd = width // ndev
    chunk = min(2048, u.shape[1])
    dma = pltpu.SemaphoreType.DMA((ndev,))
    vmem = pl.BlockSpec(memory_space=pltpu.VMEM)
    hbm = pl.BlockSpec(memory_space=pltpu.MemorySpace.HBM)
    return pl.pallas_call(
        functools.partial(gram_kernel, ndev, ns, chunk),
        out_shape=jax.ShapeDtypeStruct((width, width), jnp.float32),
        in_specs=[hbm, hbm],
        out_specs=vmem,
        scratch_shapes=[
            pltpu.VMEM(u.shape, jnp.float32),
            pltpu.VMEM(r.shape, jnp.float32),
            pltpu.VMEM((ndev, rpd, width), jnp.float32),
            pltpu.VMEM((ndev, rpd, width), jnp.float32),
            pltpu.VMEM((rpd, width), jnp.float32),
            pltpu.VMEM((ndev, rpd, width), jnp.float32),
            pltpu.SemaphoreType.DMA((u.shape[1] // chunk + 1,)),
            dma, dma, dma, dma,
        ],
        compiler_params=pltpu.CompilerParams(
            collective_id=0, has_side_effects=True, vmem_limit_bytes=60 * 1024 * 1024),
    )(u, r)


def factor_panels(sums_ref, restart_ref, work, upper, nrows, panel):
    keep, k = restart_ref.shape
    width = sums_ref.shape[1]
    row = lax.broadcasted_iota(jnp.int32, (width, width), 0)
    lane = lax.broadcasted_iota(jnp.int32, (width, width), 1)
    line = lax.broadcasted_iota(jnp.int32, (1, width), 1)
    work[:, :width] = sums_ref[...] * (1.0 / nrows)
    work[:, width:] = jnp.where(row == lane, 1.0, 0.0)
    upper[...] = jnp.zeros_like(upper)

    def step(i, carry):
        base = i * panel
        rows = [work[pl.ds(base + a, 1), :] for a in range(panel)]
        left = work[:, :width]
        cols = [jnp.sum(jnp.where(lane == base + a, left, 0.0), axis=1, keepdims=True) for a in range(panel)]
        block = {
            (a, b): jnp.sum(jnp.where(line == base + b, rows[a][:, :width], 0.0), axis=1, keepdims=True)
            for a in range(panel) for b in range(a, panel)
        }
        for a in range(panel):
            inverse = 1.0 / block[a, a]
            for b in range(a + 1, panel):
                ratio = block[a, b] * inverse
                rows[b] = rows[b] - ratio * rows[a]
                cols[b] = cols[b] - ratio * cols[a]
                for c in range(b, panel):
                    block[b, c] = block[b, c] - ratio * block[a, c]
            cols[a] = (cols[a], inverse)
            upper[pl.ds(base + a, 1), :] = rows[a] * lax.rsqrt(block[a, a])
        work[...] = work[...] - sum((cols[a][0] * cols[a][1]) * rows[a] for a in range(panel))
        return carry

    lax.fori_loop(0, k // panel, step, 0)
    both = jnp.dot(restart_ref[...], upper[:k, :], precision=HIGHEST, preferred_element_type=jnp.float32)
    half = upper[:, :width].T[k : k + 8, :]
    proj = jnp.dot(half, upper[:, width:], precision=HIGHEST, preferred_element_type=jnp.float32)
    raised = both[:, :k]
    weights = jnp.concatenate([both[:, width:], proj], axis=0)[:, :k]
    return weights, raised


def exchange_kernel(ndev, ns, keep, count, nrows, u_hbm, r_hbm, sums_ref, restart_ref, coeff_ref,
                    big_out, small_out, coeff_out, u_ref, r_ref, work, upper, load_sem, send, small, cg, own_sem,
                    s1, r1, s2, r2, s3, r3):
    r, s = lax.axis_index("rows"), lax.axis_index("sub")
    me = r * ns + s
    nr = ndev // ns
    bs = send.shape[2]
    load_u = pltpu.make_async_copy(u_hbm, u_ref, load_sem.at[0])
    load_r = pltpu.make_async_copy(r_hbm, r_ref, load_sem.at[1])
    load_u.start()
    load_r.start()
    barrier = greet_all(me, ndev, ns)

    def coeff_copy(t, slot):
        return pltpu.make_async_remote_copy(
            src_ref=coeff_ref, dst_ref=cg.at[slot], send_sem=s3.at[t], recv_sem=r3.at[slot],
            device_id=(r, t), device_id_type=MESH)

    def big_copy(j, slot):
        return pltpu.make_async_remote_copy(
            src_ref=send.at[j], dst_ref=big_out.at[slot], send_sem=s1.at[j], recv_sem=r1.at[slot],
            device_id=(j // ns, j % ns), device_id_type=MESH)

    def small_copy(j, slot):
        return pltpu.make_async_remote_copy(
            src_ref=small.at[j], dst_ref=small_out.at[slot], send_sem=s2.at[j], recv_sem=r2.at[slot],
            device_id=(j // ns, j % ns), device_id_type=MESH)

    def loop(action):
        def body(o, carry):
            action((me + o) % ndev)
            return carry
        lax.fori_loop(1, ndev, body, 0)

    panel = next(p for p in (4, 2, 1) if restart_ref.shape[1] % p == 0)
    weights, raised = factor_panels(sums_ref, restart_ref, work, upper, nrows, panel)
    load_u.wait()
    load_r.wait()
    half = ns // 2
    side, pos = s // half, s % half
    across = [(1 - side) * half + (pos + q) % half for q in range(half)]
    beside = [side * half + (pos + q) % half for q in range(half)]
    order = []
    for q in range(half):
        order += [across[q], beside[half - 1 - q]]

    def step(d, acc):
        targets = [((r + d) % nr) * ns + t for t in order]
        for j in targets:
            cols = pl.ds(pl.multiple_of(j * bs, bs), bs)
            y = jnp.dot(weights, u_ref[:, cols], precision=HIGHEST, preferred_element_type=jnp.float32)
            rest = r_ref[:, cols] - y[keep : keep + 1, :]
            send[j] = y[:keep, :]
            small[j, 0:1, :] = rest
            acc = acc + rest * rest

        @pl.when(d == 0)
        def _():
            pl.semaphore_wait(barrier, ndev - 1)

        for j in targets:
            @pl.when(j != me)
            def _():
                big_copy(j, me).start()

        return acc

    acc = lax.fori_loop(0, nr, step, jnp.zeros((1, bs), jnp.float32))
    partial = jnp.sum(acc, axis=1, keepdims=True)

    def mark(j, carry):
        small[j, 1:2, :] = jnp.broadcast_to(partial, (1, bs))
        return carry

    lax.fori_loop(0, ndev, mark, 0)
    own_big = pltpu.make_async_copy(send.at[me], big_out.at[me], own_sem.at[0])
    own_small = pltpu.make_async_copy(small.at[me], small_out.at[me], own_sem.at[1])
    own_big.start()
    own_small.start()
    for o in range(1, ns):
        coeff_copy((s + o) % ns, s).start()
    loop(lambda j: small_copy(j, me).start())
    cg[s] = coeff_ref[...]
    for o in range(1, ns):
        coeff_copy((s + o) % ns, (s + o) % ns).wait_recv()
    deg, mloc, _ = coeff_ref.shape
    turned = [
        jnp.concatenate(
            [
                lax.dot_general(raised, cg[t, i], (((1,), (1,)), ((), ())), precision=HIGHEST,
                                preferred_element_type=jnp.float32)
                for t in range(ns)
            ],
            axis=1,
        )
        for i in range(deg)
    ]
    squares = sum(jnp.sum(part * part) for part in turned)
    scale = lax.rsqrt(jnp.full((1, 1), squares / count + 1e-06, jnp.float32))
    for i in range(deg):
        coeff_out[i] = turned[i] * scale
    own_big.wait()
    own_small.wait()
    loop(lambda j: big_copy(j, j).wait_recv())
    loop(lambda j: small_copy(j, j).wait_recv())
    loop(lambda j: big_copy(j, me).wait_send())
    loop(lambda j: small_copy(j, me).wait_send())
    for o in range(1, ns):
        coeff_copy((s + o) % ns, s).wait_send()


def exchange(u, r, sums, restart, coeff_t, keep, count, ndev, ns):
    bs = u.shape[1] // ndev
    vmem = pl.BlockSpec(memory_space=pltpu.VMEM)
    hbm = pl.BlockSpec(memory_space=pltpu.MemorySpace.HBM)
    dma = pltpu.SemaphoreType.DMA((ndev,))
    few = pltpu.SemaphoreType.DMA((ns,))
    f32 = jnp.float32
    return pl.pallas_call(
        functools.partial(exchange_kernel, ndev, ns, keep, count, u.shape[1] * ndev),
        out_shape=(
            jax.ShapeDtypeStruct((ndev, keep, bs), f32),
            jax.ShapeDtypeStruct((ndev, 2, bs), f32),
            jax.ShapeDtypeStruct((coeff_t.shape[0], keep, ns * coeff_t.shape[1]), f32),
        ),
        in_specs=[hbm, hbm, vmem, vmem, vmem],
        out_specs=(hbm, hbm, vmem),
        scratch_shapes=[
            pltpu.VMEM(u.shape, f32),
            pltpu.VMEM(r.shape, f32),
            pltpu.VMEM((sums.shape[0], 2 * sums.shape[1]), f32),
            pltpu.VMEM((sums.shape[0], 2 * sums.shape[1]), f32),
            pltpu.SemaphoreType.DMA((2,)),
            pltpu.VMEM((ndev, keep, bs), f32),
            pltpu.VMEM((ndev, 2, bs), f32),
            pltpu.VMEM((ns,) + coeff_t.shape, f32),
            pltpu.SemaphoreType.DMA((2,)),
            dma, dma, dma, dma, few, few,
        ],
        compiler_params=pltpu.CompilerParams(
            collective_id=1, has_side_effects=True, vmem_limit_bytes=60 * 1024 * 1024),
    )(u, r, sums, restart, coeff_t)


def place_kernel(ndev, nrows, slots, big, small_hbm, rows_out, vec_out, held, small, in_sem, out_sem, small_sem):
    bs = held.shape[2]
    load_small = pltpu.make_async_copy(small_hbm, small, small_sem.at[0])

    def fetch(d):
        return pltpu.make_async_copy(big.at[d], held.at[d], in_sem.at[d])

    def put(d):
        cols = pl.ds(pl.multiple_of(slots[0, d] * bs, bs), bs)
        return pltpu.make_async_copy(held.at[d], rows_out.at[:, cols], out_sem.at[d])

    def loop(action):
        def body(d, carry):
            action(d)
            return carry
        lax.fori_loop(0, ndev, body, 0)

    loop(lambda d: fetch(d).start())
    load_small.start()

    def move(d):
        fetch(d).wait()
        put(d).start()

    loop(move)
    load_small.wait()
    total = jnp.sum(small[:, 1, :], axis=0, keepdims=True)
    scale = lax.rsqrt(total / nrows + 1e-06)
    for d in range(ndev):
        cols = pl.ds(pl.multiple_of(slots[0, d] * bs, bs), bs)
        vec_out[:, cols] = small[d, 0:1, :] * scale
    loop(lambda d: put(d).wait())


def place(slot_row, big, small, nrows):
    ndev, keep, bs = big.shape
    vmem = pl.BlockSpec(memory_space=pltpu.VMEM)
    hbm = pl.BlockSpec(memory_space=pltpu.MemorySpace.HBM)
    dma = pltpu.SemaphoreType.DMA((ndev,))
    return pl.pallas_call(
        functools.partial(place_kernel, ndev, nrows),
        out_shape=(
            jax.ShapeDtypeStruct((keep, ndev * bs), jnp.float32),
            jax.ShapeDtypeStruct((1, ndev * bs), jnp.float32),
        ),
        in_specs=[pl.BlockSpec(memory_space=pltpu.SMEM), hbm, hbm],
        out_specs=(hbm, vmem),
        scratch_shapes=[
            pltpu.VMEM(big.shape, jnp.float32),
            pltpu.VMEM(small.shape, jnp.float32),
            dma, dma, pltpu.SemaphoreType.DMA((1,)),
        ],
        compiler_params=pltpu.CompilerParams(vmem_limit_bytes=60 * 1024 * 1024),
    )(slot_row, big, small)


def local(u, r, slot_map, restart, coeff):
    ndev = lax.axis_size(AXES)
    ns = lax.axis_size("sub")
    k, keep = restart.shape
    nrows = u.shape[1] * ndev
    deg, _, mloc = coeff.shape
    sums = gram_sums(u, r, ndev, ns)
    coeff_t = coeff.transpose(0, 2, 1)
    big, small, new_coeff = exchange(u, r, sums, restart.T, coeff_t, keep, deg * keep * mloc * ns, ndev, ns)
    rows, vec = place(slot_map, big, small, nrows)
    return rows, vec, new_coeff


def solution(mesh):
    P = jax.sharding.PartitionSpec
    in_specs = (P(None, AXES), P(None, AXES), P(AXES, None), P(), P(None, None, "sub"))
    out_specs = (P(None, AXES), P(None, AXES), P())
    return jax.shard_map(local, mesh=mesh, in_specs=in_specs, out_specs=out_specs, check_vma=False)
```

profile of v0, /device:TPU:0, one launch (start us, length us, event | category | flops | bytes accessed | tf_op | source)
XLA Modules:
  0.0 104.3 jit_solution(14431577883136751564)
XLA Ops:
  0.6 21.4 %shard_map.76.sums_ref = f32[128,128]{1,0:T(8,128)} custom-call(f32[120,16384]{1,0:T(8,128)} %u_hbm.3, f32[1,16384]{1,0:T(1,128)} %r_hbm.3), custom_call_target="tpu_custom_call" | custom-call | tf_op jit(solution)/shard_map/pallas_call | solution.py:105
  22.0 77.2 %shard_map.77 = (f32[32,40,512]{2,1,0:T(8,128)}, f32[32,2,512]{2,1,0:T(2,128)}, f32[3,40,120]{2,1,0:T(8,128)}) custom-call(f32[120,16384]{1,0:T(8,128)} %u_hbm.3, f32[1,16384]{1,0:T(1,128)} %r_hbm.3, f32[128,128]{1,0:T(8,128)} %shard_map.76.sums_ref, f32[40,120]{1,0:T(8,128)} %bitcast.3, f32[3,30,120]{2,1,0:T(8,128)} %bitcast.2), custom_call_target="tpu_custom_call" | custom-call | tf_op jit(solution)/shard_map/pallas_call | solution.py:284
  99.2 0.0 copy-start
  99.2 4.5 %shard_map.78 = (f32[40,16384]{1,0:T(8,128)}, f32[1,16384]{1,0:T(1,128)}) custom-call(s32[1,32]{1,0:T(1,128)} %slots.1, f32[32,40,512]{2,1,0:T(8,128)} %get-tuple-element.8.big, f32[32,2,512]{2,1,0:T(2,128)} %get-tuple-element.9.small_hbm), custom_call_target="tpu_custom_call" | custom-call | tf_op jit(solution)/shard_map/pallas_call | solution.py:349
  103.7 0.0 copy-done
  103.7 0.6 copy.9
Async XLA Ops:
  99.2 4.5 %copy-start = (f32[3,40,120]{2,1,0:T(8,128)S(1)}, f32[3,40,120]{2,1,0:T(8,128)}, u32[]{:S(2)}) copy-start(f32[3,40,120]{2,1,0:T(8,128)} %get-tuple-element.18) | copy-start | bytes 172804
where the time goes:
time: 105 us; the launch traced here: 104 us
  Pallas kernels  103 us (98%)
    pallas_call x1, Pallas kernels, exchange(): pl.pallas_call(functools.partial(exchange_kernel, ndev, ns, keep, count,...  77.2 us
    pallas_call x1, Pallas kernels, gram_sums(): pl.pallas_call(functools.partial(gram_kernel, ndev, ns, chunk), out_shape...  21.4 us
    pallas_call x1, Pallas kernels, place(): pl.pallas_call(functools.partial(place_kernel, ndev, nrows), out_shape=(j...  4.46 us

commit v1 on v0

v1 whole, which is shorter than its diff:
```python
import functools

import jax
import jax.numpy as jnp
from jax import lax
from jax.experimental import pallas as pl
from jax.experimental.pallas import tpu as pltpu

HIGHEST = lax.Precision.HIGHEST
MESH = pl.DeviceIdType.MESH
AXES = ("rows", "sub")
LANES = 128
SUBLANES = 8


def greet_all(me, ndev, ns):
    barrier = pltpu.get_barrier_semaphore()

    def greet(o, carry):
        j = (me + o) % ndev
        pl.semaphore_signal(barrier, inc=1, device_id=(j // ns, j % ns), device_id_type=MESH)
        return carry

    lax.fori_loop(1, ndev, greet, 0)
    return barrier


def gram_piece(u_ref, r_ref, col, chunk):
    cols = pl.ds(col, chunk)
    pad = LANES - u_ref.shape[0]
    first = lax.broadcasted_iota(jnp.int32, (pad, chunk), 0) == 0
    tail = jnp.where(first, jnp.broadcast_to(r_ref[:, cols], (pad, chunk)), 0.0)
    x = jnp.concatenate([u_ref[:, cols], tail], axis=0)
    hi = x.astype(jnp.bfloat16)
    lo = (x - hi.astype(jnp.float32)).astype(jnp.bfloat16)
    both = jnp.concatenate([hi, lo], axis=0)
    return lax.dot_general(both, both, (((1,), (1,)), ((), ())), preferred_element_type=jnp.float32)


def factor_panels(sums_ref, restart_ref, work, upper, nrows, panel):
    keep, k = restart_ref.shape
    width = sums_ref.shape[1]
    row = lax.broadcasted_iota(jnp.int32, (width, width), 0)
    lane = lax.broadcasted_iota(jnp.int32, (width, width), 1)
    line = lax.broadcasted_iota(jnp.int32, (1, width), 1)
    work[:, :width] = sums_ref[...] * (1.0 / nrows)
    work[:, width:] = jnp.where(row == lane, 1.0, 0.0)
    upper[...] = jnp.zeros_like(upper)

    def step(i, carry):
        base = i * panel
        rows = [work[pl.ds(base + a, 1), :] for a in range(panel)]
        left = work[:, :width]
        cols = [jnp.sum(jnp.where(lane == base + a, left, 0.0), axis=1, keepdims=True) for a in range(panel)]
        block = {
            (a, b): jnp.sum(jnp.where(line == base + b, rows[a][:, :width], 0.0), axis=1, keepdims=True)
            for a in range(panel) for b in range(a, panel)
        }
        for a in range(panel):
            inverse = 1.0 / block[a, a]
            for b in range(a + 1, panel):
                ratio = block[a, b] * inverse
                rows[b] = rows[b] - ratio * rows[a]
                cols[b] = cols[b] - ratio * cols[a]
                for c in range(b, panel):
                    block[b, c] = block[b, c] - ratio * block[a, c]
            cols[a] = (cols[a], inverse)
            upper[pl.ds(base + a, 1), :] = rows[a] * lax.rsqrt(block[a, a])
        work[...] = work[...] - sum((cols[a][0] * cols[a][1]) * rows[a] for a in range(panel))
        return carry

    lax.fori_loop(0, k // panel, step, 0)
    both = jnp.dot(restart_ref[...], upper[:k, :], precision=HIGHEST, preferred_element_type=jnp.float32)
    half = upper[:, :width].T[k : k + 8, :]
    proj = jnp.dot(half, upper[:, width:], precision=HIGHEST, preferred_element_type=jnp.float32)
    raised = both[:, :k]
    weights = jnp.concatenate([both[:, width:], proj], axis=0)[:, :k]
    return weights, raised


def restart_kernel(ndev, ns, count, nrows, chunk, u_hbm, r_hbm, restart_hbm, coeff_hbm,
                   big, small, coeff_out, u_ref, r_ref, restart_ref, coeff_ref, part, gathered, red, sums, work, upper, weights_ref,
                   send, row_send, turn_send, turn_mid, turn_all, load_sem, own_sem,
                   s1, r1, s2, r2, s3, r3, s4, r4, s5, r5, s6, r6):
    r, s = lax.axis_index("rows"), lax.axis_index("sub")
    me = r * ns + s
    nr = ndev // ns
    keep, k = restart_ref.shape
    bs = send.shape[2]
    deg, mloc, _ = coeff_ref.shape
    pieces = u_ref.shape[1] // chunk

    def remote(src, dst, send_sem, recv_sem, dev):
        return pltpu.make_async_remote_copy(
            src_ref=src, dst_ref=dst, send_sem=send_sem, recv_sem=recv_sem, device_id=dev, device_id_type=MESH)

    def others(action):
        def body(o, carry):
            action((me + o) % ndev)
            return carry
        lax.fori_loop(1, ndev, body, 0)

    load_r = pltpu.make_async_copy(r_hbm, r_ref, load_sem.at[pieces])
    load_r.start()
    load_small = [pltpu.make_async_copy(restart_hbm, restart_ref, own_sem.at[0]),
                  pltpu.make_async_copy(coeff_hbm, coeff_ref, own_sem.at[1])]
    loads = []
    for c in range(pieces):
        cols = pl.ds(c * chunk, chunk)
        loads.append(pltpu.make_async_copy(u_hbm.at[:, cols], u_ref.at[:, cols], load_sem.at[c]))
        loads[-1].start()
    for load in load_small:
        load.start()
    barrier = greet_all(me, ndev, ns)

    load_r.wait()
    full = jnp.zeros((2 * LANES, 2 * LANES), jnp.float32)
    for c in range(pieces):
        loads[c].wait()
        full = full + gram_piece(u_ref, r_ref, c * chunk, chunk)
    cross = full[:LANES, LANES:]
    part[...] = full[:LANES, :LANES] + (cross + cross.T) + full[LANES:, LANES:]
    pl.semaphore_wait(barrier, ndev - 1)

    groups = part.shape[0] // SUBLANES
    middle = ns - 2 * (ns // 4)
    own = r * middle + s - ns // 4
    owning = (s >= ns // 4) & (s < ns // 4 + middle) & (own < groups)

    def owner(g):
        return g // middle, ns // 4 + g % middle

    def group_rows(ref, g):
        return ref.at[pl.ds(pl.multiple_of(g * SUBLANES, SUBLANES), SUBLANES), :]

    def scatter_copy(g, slot):
        return remote(group_rows(part, g), gathered.at[slot], s1.at[g], r1.at[slot], owner(g))

    def gather_copy(j, g):
        return remote(red, group_rows(sums, g), s2.at[j], r2.at[g], (j // ns, j % ns))

    def groups_not_mine(action):
        def body(o, carry):
            g = (r * middle + o) % groups
            @pl.when(jnp.logical_not(owning & (g == own)))
            def _():
                action(g)
            return carry
        lax.fori_loop(0, groups, body, 0)

    groups_not_mine(lambda g: scatter_copy(g, me).start())

    @pl.when(owning)
    def _():
        mine = pl.ds(pl.multiple_of(own * SUBLANES, SUBLANES), SUBLANES)
        others(lambda j: scatter_copy(own, j).wait_recv())
        gathered[me] = part[mine, :]
        total = jnp.sum(gathered[...], axis=0)
        red[...] = total
        sums[mine, :] = total
        others(lambda j: gather_copy(j, own).start())

    groups_not_mine(lambda g: gather_copy(me, g).wait_recv())

    for load in load_small:
        load.wait()
    panel = next(p for p in (4, 2, 1) if k % p == 0)
    weights, raised = factor_panels(sums, restart_ref, work, upper, nrows, panel)
    weights_ref[...] = weights

    def big_copy(j, slot):
        return remote(send.at[j], big.at[slot], s3.at[j], r3.at[slot], (j // ns, j % ns))

    def small_copy(j, slot):
        return remote(row_send.at[j], small.at[slot], s4.at[j], r4.at[slot], (j // ns, j % ns))

    half = ns // 2
    side, pos = s // half, s % half
    across = [(1 - side) * half + (pos + q) % half for q in range(half)]
    beside = [side * half + (pos + q) % half for q in range(half)]
    order = []
    for q in range(half):
        order += [across[q], beside[half - 1 - q]]

    def step(d, acc):
        for t in order:
            j = ((r + d) % nr) * ns + t
            cols = pl.ds(pl.multiple_of(j * bs, bs), bs)
            y = jnp.dot(weights_ref[...], u_ref[:, cols], precision=HIGHEST, preferred_element_type=jnp.float32)
            rest = r_ref[:, cols] - y[keep : keep + 1, :]
            row_send[j, 0:1, :bs] = rest
            acc = acc + rest * rest

            @pl.when(j != me)
            def _():
                send[j] = y[:keep, :]
                big_copy(j, me).start()

            @pl.when(j == me)
            def _():
                big[me] = y[:keep, :]

        return acc

    acc = step(0, jnp.zeros((1, bs), jnp.float32))

    width = turn_send.shape[1]
    turn_send[...] = jnp.zeros_like(turn_send)
    for i in range(deg):
        turned = lax.dot_general(coeff_ref[i], raised, (((1,), (1,)), ((), ())), precision=HIGHEST,
                                 preferred_element_type=jnp.float32)
        turn_send[:mloc, i * keep : (i + 1) * keep] = turned
    share = turn_mid.shape[1]
    my_rows = pl.ds(pl.multiple_of(r * share, share), share)
    for i in range(nr):
        @pl.when(r == i)
        def _():
            turn_mid[s] = turn_send[i * share : (i + 1) * share, :]

    def turn_copy(t, slot):
        return remote(turn_mid.at[s], turn_mid.at[slot], s5.at[t], r5.at[slot], (r, t))

    def spread_copy(p, slot):
        return remote(turn_mid, turn_all.at[slot], s6.at[p], r6.at[slot], (p, s))

    def along(action):
        for o in range(1, ns):
            action((s + o) % ns)

    def plane(action):
        def body(o, carry):
            action((r + o) % nr)
            return carry
        lax.fori_loop(1, nr, body, 0)

    along(lambda t: turn_copy(t, s).start())
    acc = lax.fori_loop(1, nr, step, acc)
    partial = jnp.sum(acc, axis=1, keepdims=True)

    def mark(j, carry):
        row_send[j, 0:1, bs:] = jnp.broadcast_to(partial, (1, LANES))
        return carry

    lax.fori_loop(0, ndev, mark, 0)
    others(lambda j: small_copy(j, me).start())
    small[me] = row_send[me]
    along(lambda t: turn_copy(t, t).wait_recv())
    plane(lambda p: spread_copy(p, r).start())
    turn_all[r] = turn_mid[...]
    plane(lambda p: spread_copy(p, p).wait_recv())
    columns = []
    for t in range(ns):
        columns.append(jnp.concatenate([turn_all[p, t] for p in range(nr)], axis=0)[:mloc, :])
    turned = jnp.concatenate(columns, axis=0).T
    squares = jnp.sum(turned * turned)
    scale = lax.rsqrt(jnp.full((1, 1), squares / count + 1e-06, jnp.float32))
    for i in range(deg):
        coeff_out[i] = turned[i * keep : (i + 1) * keep, :] * scale

    others(lambda j: big_copy(j, j).wait_recv())
    others(lambda j: small_copy(j, j).wait_recv())
    groups_not_mine(lambda g: scatter_copy(g, me).wait_send())

    @pl.when(owning)
    def _():
        others(lambda j: gather_copy(j, own).wait_send())

    others(lambda j: big_copy(j, me).wait_send())
    others(lambda j: small_copy(j, me).wait_send())
    along(lambda t: turn_copy(t, s).wait_send())
    plane(lambda p: spread_copy(p, r).wait_send())


def restart_call(u, r, restart, coeff_t, ndev, ns):
    f32 = jnp.float32
    bs = u.shape[1] // ndev
    nr = ndev // ns
    keep, k = restart.shape
    deg, mloc, _ = coeff_t.shape
    count = deg * keep * mloc * ns
    chunk = min(2048, u.shape[1])
    groups = LANES // SUBLANES
    share = -(-mloc // nr)
    lanes = -(-deg * keep // LANES) * LANES
    vmem = pl.BlockSpec(memory_space=pltpu.VMEM)
    hbm = pl.BlockSpec(memory_space=pltpu.MemorySpace.HBM)
    dma = pltpu.SemaphoreType.DMA
    return pl.pallas_call(
        functools.partial(restart_kernel, ndev, ns, count, u.shape[1] * ndev, chunk),
        out_shape=(
            pltpu.VMEM((ndev, keep, bs), f32),
            pltpu.VMEM((ndev, 1, bs + LANES), f32),
            pltpu.VMEM((deg, keep, ns * mloc), f32),
        ),
        in_specs=[hbm, hbm, hbm, hbm],
        out_specs=(vmem, vmem, vmem),
        scratch_shapes=[
            pltpu.VMEM(u.shape, f32),
            pltpu.VMEM(r.shape, f32),
            pltpu.VMEM(restart.shape, f32),
            pltpu.VMEM(coeff_t.shape, f32),
            pltpu.VMEM((LANES, LANES), f32),
            pltpu.VMEM((ndev, SUBLANES, LANES), f32),
            pltpu.VMEM((SUBLANES, LANES), f32),
            pltpu.VMEM((LANES, LANES), f32),
            pltpu.VMEM((LANES, 2 * LANES), f32),
            pltpu.VMEM((LANES, 2 * LANES), f32),
            pltpu.VMEM((keep + SUBLANES, k), f32),
            pltpu.VMEM((ndev, keep, bs), f32),
            pltpu.VMEM((ndev, 1, bs + LANES), f32),
            pltpu.VMEM((nr * share, lanes), f32),
            pltpu.VMEM((ns, share, lanes), f32),
            pltpu.VMEM((nr, ns, share, lanes), f32),
            dma((u.shape[1] // chunk + 1,)),
            dma((2,)),
            dma((groups,)), dma((ndev,)),
            dma((ndev,)), dma((groups,)),
            dma((ndev,)), dma((ndev,)),
            dma((ndev,)), dma((ndev,)),
            dma((ns,)), dma((ns,)),
            dma((nr,)), dma((nr,)),
        ],
        compiler_params=pltpu.CompilerParams(
            collective_id=0, has_side_effects=True, vmem_limit_bytes=48 * 1024 * 1024),
    )(*[pltpu.with_memory_space_constraint(a, pltpu.MemorySpace.HBM) for a in (u, r, restart, coeff_t)])


def place_kernel(ndev, nrows, slots, big, small, coeff, rows_out, vec_out, coeff_out, out_sem):
    bs = big.shape[2]

    def put(d):
        cols = pl.ds(pl.multiple_of(slots[0, d] * bs, bs), bs)
        return pltpu.make_async_copy(big.at[d], rows_out.at[:, cols], out_sem.at[d])

    def loop(action):
        def body(d, carry):
            action(d)
            return carry
        lax.fori_loop(0, ndev, body, 0)

    loop(lambda d: put(d).start())
    total = jnp.sum(small[:, 0, bs : bs + LANES], axis=0, keepdims=True)[:, :1]
    scale = lax.rsqrt(total / nrows + 1e-06)
    for d in range(ndev):
        cols = pl.ds(pl.multiple_of(slots[0, d] * bs, bs), bs)
        vec_out[:, cols] = small[d, 0:1, :bs] * scale
    coeff_out[...] = coeff[...]
    loop(lambda d: put(d).wait())


def place(slot_row, big, small, coeff, nrows):
    ndev, keep, bs = big.shape
    vmem = pl.BlockSpec(memory_space=pltpu.VMEM)
    hbm = pl.BlockSpec(memory_space=pltpu.MemorySpace.HBM)
    return pl.pallas_call(
        functools.partial(place_kernel, ndev, nrows),
        out_shape=(
            jax.ShapeDtypeStruct((keep, ndev * bs), jnp.float32),
            jax.ShapeDtypeStruct((1, ndev * bs), jnp.float32),
            jax.ShapeDtypeStruct(coeff.shape, jnp.float32),
        ),
        in_specs=[pl.BlockSpec(memory_space=pltpu.SMEM), vmem, vmem, vmem],
        out_specs=(hbm, vmem, vmem),
        scratch_shapes=[pltpu.SemaphoreType.DMA((ndev,))],
        compiler_params=pltpu.CompilerParams(vmem_limit_bytes=32 * 1024 * 1024),
    )(slot_row, big, small, coeff)


def local(u, r, slot_map, restart, coeff):
    ndev = lax.axis_size(AXES)
    ns = lax.axis_size("sub")
    nrows = u.shape[1] * ndev
    big, small, new_coeff = restart_call(u, r, restart.T, coeff.transpose(0, 2, 1), ndev, ns)
    return place(slot_map, big, small, new_coeff, nrows)


def solution(mesh):
    P = jax.sharding.PartitionSpec
    in_specs = (P(None, AXES), P(None, AXES), P(AXES, None), P(), P(None, None, "sub"))
    out_specs = (P(None, AXES), P(None, AXES), P())
    return jax.shard_map(local, mesh=mesh, in_specs=in_specs, out_specs=out_specs, check_vma=False)
```

time: 105 us -> 93.2 us (0.89)
  Pallas kernels: 103 us -> 92.4 us
    pallas_call x2 -> x1, Pallas kernels: 98.5 us -> 89.5 us  [restart_call(): pl.pallas_call(functools.partial(restart_kernel, ndev, ns, count, u.shape...]
    pallas_call x1, Pallas kernels: 4.46 us -> 2.95 us  [place(): pl.pallas_call(functools.partial(place_kernel, ndev, nrows), out_shape=(j...]
where the time goes in v1:
time: 93.2 us; the launch traced here: 93.1 us
  Pallas kernels  92.4 us (99%)
    pallas_call x1, Pallas kernels, restart_call(): pl.pallas_call(functools.partial(restart_kernel, ndev, ns, count, u.shape...  89.5 us
    pallas_call x1, Pallas kernels, place(): pl.pallas_call(functools.partial(place_kernel, ndev, nrows), out_shape=(j...  2.95 us

profile of v1, /device:TPU:0, one launch (start us, length us, event | category | flops | bytes accessed | tf_op | source)
XLA Modules:
  0.0 93.1 jit_solution(6105213338701142607)
XLA Ops:
  0.6 0.0 copy-start
  0.6 89.5 %shard_map.76 = (f32[32,40,512]{2,1,0:T(8,128)S(1)}, f32[32,1,640]{2,1,0:T(1,128)S(1)}, f32[3,40,120]{2,1,0:T(8,128)S(1)}) custom-call(f32[120,16384]{1,0:T(8,128)} %u_hbm.1, f32[1,16384]{1,0:T(1,128)} %r_hbm.1, f32[40,120]{1,0:T(8,128)} %bitcast.3, f32[3,30,120]{2,1,0:T(8,128)} %bitcast.2), custom_call_target="tpu_custom_call" | custom-call | tf_op jit(solution)/shard_map/pallas_call | solution.py:288
  90.1 0.0 copy-done
  90.1 2.9 %shard_map.77 = (f32[40,16384]{1,0:T(8,128)}, f32[1,16384]{1,0:T(1,128)}, f32[3,40,120]{2,1,0:T(8,128)}) custom-call(s32[1,32]{1,0:T(1,128)S(1)} %copy-done, f32[32,40,512]{2,1,0:T(8,128)S(1)} %get-tuple-element.6.big, f32[32,1,640]{2,1,0:T(1,128)S(1)} %get-tuple-element.7.small, f32[3,40,120]{2,1,0:T(8,128)S(1)} %get-tuple-element.8.coeff), custom_call_target="tpu_custom_call" | custom-call | tf_op jit(solution)/shard_map/pallas_call | solution.py:355
Async XLA Ops:
  0.6 89.5 %copy-start = (s32[1,32]{1,0:T(1,128)S(1)}, s32[1,32]{1,0:T(1,128)}, u32[]{:S(2)}) copy-start(s32[1,32]{1,0:T(1,128)} %slots.1) | copy-start | bytes 388

commit v2 on v1

--- a/solution.py
+++ b/solution.py
@@ -11,6 +11,7 @@
 AXES = ("rows", "sub")
 LANES = 128
 SUBLANES = 8
+RAW_BLOCKS = 2
 
 
 def greet_all(me, ndev, ns):
@@ -33,8 +34,9 @@
     x = jnp.concatenate([u_ref[:, cols], tail], axis=0)
     hi = x.astype(jnp.bfloat16)
     lo = (x - hi.astype(jnp.float32)).astype(jnp.bfloat16)
-    both = jnp.concatenate([hi, lo], axis=0)
-    return lax.dot_general(both, both, (((1,), (1,)), ((), ())), preferred_element_type=jnp.float32)
+    dims = (((1,), (1,)), ((), ()))
+    return (lax.dot_general(hi, hi, dims, preferred_element_type=jnp.float32),
+            lax.dot_general(hi, lo, dims, preferred_element_type=jnp.float32))
 
 
 def factor_panels(sums_ref, restart_ref, work, upper, nrows, panel):
@@ -78,10 +80,10 @@
     return weights, raised
 
 
-def restart_kernel(ndev, ns, count, nrows, chunk, u_hbm, r_hbm, restart_hbm, coeff_hbm,
-                   big, small, coeff_out, u_ref, r_ref, restart_ref, coeff_ref, part, gathered, red, sums, work, upper, weights_ref,
-                   send, row_send, turn_send, turn_mid, turn_all, load_sem, own_sem,
-                   s1, r1, s2, r2, s3, r3, s4, r4, s5, r5, s6, r6):
+def restart_kernel(ndev, ns, count, nrows, chunk, raw, u_hbm, r_hbm, restart_hbm, coeff_hbm,
+                   big, small, coeff_out, u_ref, r_ref, restart_ref, coeff_ref, part, gathered, mine_ref, other_ref, red, sums, work, upper, weights_ref,
+                   send, row_send, turn_send, turn_mid, turn_all, raw_ref, load_sem, own_sem,
+                   s1, r1, s2, r2, s3, r3, s4, r4, s5, r5, s6, r6, s7, r7):
     r, s = lax.axis_index("rows"), lax.axis_index("sub")
     me = r * ns + s
     nr = ndev // ns
@@ -114,53 +116,112 @@
     barrier = greet_all(me, ndev, ns)
 
     load_r.wait()
-    full = jnp.zeros((2 * LANES, 2 * LANES), jnp.float32)
+    main = jnp.zeros((LANES, LANES), jnp.float32)
+    cross = jnp.zeros((LANES, LANES), jnp.float32)
     for c in range(pieces):
         loads[c].wait()
-        full = full + gram_piece(u_ref, r_ref, c * chunk, chunk)
-    cross = full[:LANES, LANES:]
-    part[...] = full[:LANES, :LANES] + (cross + cross.T) + full[LANES:, LANES:]
+        one, two = gram_piece(u_ref, r_ref, c * chunk, chunk)
+        main = main + one
+        cross = cross + two
+    part[...] = main + (cross + cross.T)
     pl.semaphore_wait(barrier, ndev - 1)
 
-    groups = part.shape[0] // SUBLANES
-    middle = ns - 2 * (ns // 4)
-    own = r * middle + s - ns // 4
-    owning = (s >= ns // 4) & (s < ns // 4 + middle) & (own < groups)
+    half = ns // 2
+    side, pos = s // half, s % half
+    here = r * half + pos
+    size = red.shape[0]
+    groups = part.shape[0] // size
+    own = (r // 2) * half + pos
+    owning = (r % 2 == 1) & (own < groups)
+    opposite = (r, (s + half) % ns)
+
+    def member(m):
+        return m // half, side * half + m % half
 
     def owner(g):
-        return g // middle, ns // 4 + g % middle
+        return 2 * (g // half) + 1, side * half + g % half
 
     def group_rows(ref, g):
-        return ref.at[pl.ds(pl.multiple_of(g * SUBLANES, SUBLANES), SUBLANES), :]
+        return ref.at[pl.ds(pl.multiple_of(g * size, size), size), :]
 
     def scatter_copy(g, slot):
         return remote(group_rows(part, g), gathered.at[slot], s1.at[g], r1.at[slot], owner(g))
 
-    def gather_copy(j, g):
-        return remote(red, group_rows(sums, g), s2.at[j], r2.at[g], (j // ns, j % ns))
+    def cross_copy():
+        return remote(mine_ref, other_ref, s2.at[nr * half], r2.at[groups], opposite)
+
+    def gather_copy(m, g):
+        return remote(red, group_rows(sums, g), s2.at[m], r2.at[g], member(m))
 
     def groups_not_mine(action):
         def body(o, carry):
-            g = (r * middle + o) % groups
+            g = (r // 2 * half + o) % groups
             @pl.when(jnp.logical_not(owning & (g == own)))
             def _():
                 action(g)
             return carry
         lax.fori_loop(0, groups, body, 0)
 
-    groups_not_mine(lambda g: scatter_copy(g, me).start())
+    def half_others(action):
+        def body(o, carry):
+            action((here + o) % (nr * half))
+            return carry
+        lax.fori_loop(1, nr * half, body, 0)
+
+    groups_not_mine(lambda g: scatter_copy(g, here).start())
+
+    inner = (s == half - 1) | (s == half)
+    facing = ns - 1 - s
+
+    def raw_peer(q):
+        return (r // 2 * 2 + (r + q) % 2 + q // 2 * 2) % nr
+
+    def raw_source(q):
+        return (r // 2 * 2 + (r + q) % 2 - q // 2 * 2 + nr) % nr
+
+    def raw_copies(q):
+        t = raw_peer(q)
+        copies = []
+        for c in range(bs // LANES):
+            cols = pl.ds(pl.multiple_of((t * ns + facing) * bs, LANES) + c * LANES, LANES)
+            copies.append(remote(u_ref.at[:, cols], raw_ref.at[q, :, pl.ds(c * LANES, LANES)],
+                                 s7.at[q, c], r7.at[q, c], (t, facing)))
+        return copies
+
+    def raw_start():
+        for q in range(raw):
+            for copy in raw_copies(q):
+                copy.start()
+
+    def is_raw(j, peer):
+        hit = j == peer(0) * ns + facing
+        for q in range(1, raw):
+            hit = hit | (j == peer(q) * ns + facing)
+        return inner & hit
+
+    @pl.when(inner & jnp.logical_not(owning))
+    def _():
+        raw_start()
 
     @pl.when(owning)
     def _():
-        mine = pl.ds(pl.multiple_of(own * SUBLANES, SUBLANES), SUBLANES)
-        others(lambda j: scatter_copy(own, j).wait_recv())
-        gathered[me] = part[mine, :]
+        mine = pl.ds(pl.multiple_of(own * size, size), size)
+        half_others(lambda m: scatter_copy(own, m).wait_recv())
+        gathered[here] = part[mine, :]
         total = jnp.sum(gathered[...], axis=0)
+        mine_ref[...] = total
+        cross_copy().start()
+        cross_copy().wait_recv()
+        total = total + other_ref[...]
         red[...] = total
         sums[mine, :] = total
-        others(lambda j: gather_copy(j, own).start())
-
-    groups_not_mine(lambda g: gather_copy(me, g).wait_recv())
+        half_others(lambda m: gather_copy(m, own).start())
+
+    @pl.when(inner & owning)
+    def _():
+        raw_start()
+
+    groups_not_mine(lambda g: gather_copy(here, g).wait_recv())
 
     for load in load_small:
         load.wait()
@@ -174,35 +235,43 @@
     def small_copy(j, slot):
         return remote(row_send.at[j], small.at[slot], s4.at[j], r4.at[slot], (j // ns, j % ns))
 
-    half = ns // 2
-    side, pos = s // half, s % half
     across = [(1 - side) * half + (pos + q) % half for q in range(half)]
     beside = [side * half + (pos + q) % half for q in range(half)]
     order = []
     for q in range(half):
-        order += [across[q], beside[half - 1 - q]]
+        order += [(across[q], True), (beside[half - 1 - q], False)]
+
+    def project(j, acc):
+        cols = pl.ds(pl.multiple_of(j * bs, bs), bs)
+        y = jnp.dot(weights_ref[...], u_ref[:, cols], precision=HIGHEST, preferred_element_type=jnp.float32)
+        rest = r_ref[:, cols] - y[keep : keep + 1, :]
+        row_send[j, 0:1, :bs] = rest
+        return y[:keep, :], acc + rest * rest
+
+    def send_block(j, is_across):
+        if is_across:
+            @pl.when(jnp.logical_not(is_raw(j, raw_peer)))
+            def _():
+                big_copy(j, me).start()
+        else:
+            big_copy(j, me).start()
 
     def step(d, acc):
-        for t in order:
+        for t, is_across in order:
             j = ((r + d) % nr) * ns + t
-            cols = pl.ds(pl.multiple_of(j * bs, bs), bs)
-            y = jnp.dot(weights_ref[...], u_ref[:, cols], precision=HIGHEST, preferred_element_type=jnp.float32)
-            rest = r_ref[:, cols] - y[keep : keep + 1, :]
-            row_send[j, 0:1, :bs] = rest
-            acc = acc + rest * rest
-
-            @pl.when(j != me)
-            def _():
-                send[j] = y[:keep, :]
-                big_copy(j, me).start()
-
-            @pl.when(j == me)
-            def _():
-                big[me] = y[:keep, :]
-
+            send[j], acc = project(j, acc)
+            send_block(j, is_across)
         return acc
 
-    acc = step(0, jnp.zeros((1, bs), jnp.float32))
+    def last_step(acc):
+        for t, is_across in order[:-1]:
+            j = r * ns + t
+            send[j], acc = project(j, acc)
+            send_block(j, is_across)
+        big[me], acc = project(me, acc)
+        return acc
+
+    acc = step(1, jnp.zeros((1, bs), jnp.float32))
 
     width = turn_send.shape[1]
     turn_send[...] = jnp.zeros_like(turn_send)
@@ -234,7 +303,8 @@
         lax.fori_loop(1, nr, body, 0)
 
     along(lambda t: turn_copy(t, s).start())
-    acc = lax.fori_loop(1, nr, step, acc)
+    acc = lax.fori_loop(2, nr, step, acc)
+    acc = last_step(acc)
     partial = jnp.sum(acc, axis=1, keepdims=True)
 
     def mark(j, carry):
@@ -244,6 +314,15 @@
     lax.fori_loop(0, ndev, mark, 0)
     others(lambda j: small_copy(j, me).start())
     small[me] = row_send[me]
+
+    @pl.when(inner)
+    def _():
+        for q in range(raw):
+            for copy in raw_copies(q):
+                copy.wait_recv()
+            y = jnp.dot(weights_ref[:keep, :], raw_ref[q], precision=HIGHEST, preferred_element_type=jnp.float32)
+            big[raw_source(q) * ns + facing] = y
+
     along(lambda t: turn_copy(t, t).wait_recv())
     plane(lambda p: spread_copy(p, r).start())
     turn_all[r] = turn_mid[...]
@@ -257,15 +336,29 @@
     for i in range(deg):
         coeff_out[i] = turned[i * keep : (i + 1) * keep, :] * scale
 
-    others(lambda j: big_copy(j, j).wait_recv())
+    def others_cooked(peer, action):
+        def body(j):
+            @pl.when(jnp.logical_not(is_raw(j, peer)))
+            def _():
+                action(j)
+        others(body)
+
+    others_cooked(raw_source, lambda j: big_copy(j, j).wait_recv())
     others(lambda j: small_copy(j, j).wait_recv())
-    groups_not_mine(lambda g: scatter_copy(g, me).wait_send())
+    groups_not_mine(lambda g: scatter_copy(g, here).wait_send())
 
     @pl.when(owning)
     def _():
-        others(lambda j: gather_copy(j, own).wait_send())
-
-    others(lambda j: big_copy(j, me).wait_send())
+        cross_copy().wait_send()
+        half_others(lambda m: gather_copy(m, own).wait_send())
+
+    @pl.when(inner)
+    def _():
+        for q in range(raw):
+            for copy in raw_copies(q):
+                copy.wait_send()
+
+    others_cooked(raw_peer, lambda j: big_copy(j, me).wait_send())
     others(lambda j: small_copy(j, me).wait_send())
     along(lambda t: turn_copy(t, s).wait_send())
     plane(lambda p: spread_copy(p, r).wait_send())
@@ -279,14 +372,15 @@
     deg, mloc, _ = coeff_t.shape
     count = deg * keep * mloc * ns
     chunk = min(2048, u.shape[1])
-    groups = LANES // SUBLANES
+    size = 2 * SUBLANES
+    groups = LANES // size
     share = -(-mloc // nr)
     lanes = -(-deg * keep // LANES) * LANES
     vmem = pl.BlockSpec(memory_space=pltpu.VMEM)
     hbm = pl.BlockSpec(memory_space=pltpu.MemorySpace.HBM)
     dma = pltpu.SemaphoreType.DMA
     return pl.pallas_call(
-        functools.partial(restart_kernel, ndev, ns, count, u.shape[1] * ndev, chunk),
+        functools.partial(restart_kernel, ndev, ns, count, u.shape[1] * ndev, chunk, RAW_BLOCKS),
         out_shape=(
             pltpu.VMEM((ndev, keep, bs), f32),
             pltpu.VMEM((ndev, 1, bs + LANES), f32),
@@ -300,8 +394,10 @@
             pltpu.VMEM(restart.shape, f32),
             pltpu.VMEM(coeff_t.shape, f32),
             pltpu.VMEM((LANES, LANES), f32),
-            pltpu.VMEM((ndev, SUBLANES, LANES), f32),
-            pltpu.VMEM((SUBLANES, LANES), f32),
+            pltpu.VMEM((ndev // 2, size, LANES), f32),
+            pltpu.VMEM((size, LANES), f32),
+            pltpu.VMEM((size, LANES), f32),
+            pltpu.VMEM((size, LANES), f32),
             pltpu.VMEM((LANES, LANES), f32),
             pltpu.VMEM((LANES, 2 * LANES), f32),
             pltpu.VMEM((LANES, 2 * LANES), f32),
@@ -311,14 +407,16 @@
             pltpu.VMEM((nr * share, lanes), f32),
             pltpu.VMEM((ns, share, lanes), f32),
             pltpu.VMEM((nr, ns, share, lanes), f32),
+            pltpu.VMEM((RAW_BLOCKS, k, bs), f32),
             dma((u.shape[1] // chunk + 1,)),
             dma((2,)),
-            dma((groups,)), dma((ndev,)),
-            dma((ndev,)), dma((groups,)),
+            dma((groups,)), dma((ndev // 2,)),
+            dma((ndev // 2 + 1,)), dma((groups + 1,)),
             dma((ndev,)), dma((ndev,)),
             dma((ndev,)), dma((ndev,)),
             dma((ns,)), dma((ns,)),
             dma((nr,)), dma((nr,)),
+            dma((RAW_BLOCKS, bs // LANES)), dma((RAW_BLOCKS, bs // LANES)),
         ],
         compiler_params=pltpu.CompilerParams(
             collective_id=0, has_side_effects=True, vmem_limit_bytes=48 * 1024 * 1024),

time: 93.2 us -> 87.2 us (0.936)
  Pallas kernels: 92.4 us -> 86.4 us
    pallas_call x1, Pallas kernels: 89.5 us -> 83.5 us  [restart_call(): pl.pallas_call(functools.partial(restart_kernel, ndev, ns, count, u.shape...]
where the time goes in v2:
time: 87.2 us; the launch traced here: 87.1 us
  Pallas kernels  86.4 us (99%)
    pallas_call x1, Pallas kernels, restart_call(): pl.pallas_call(functools.partial(restart_kernel, ndev, ns, count, u.shape...  83.5 us
    pallas_call x1, Pallas kernels, place(): pl.pallas_call(functools.partial(place_kernel, ndev, nrows), out_shape=(j...  2.95 us

profile of v2, /device:TPU:0, one launch (start us, length us, event | category | flops | bytes accessed | tf_op | source)
XLA Modules:
  0.0 87.1 jit_solution(5519284577316142885)
XLA Ops:
  0.6 0.0 copy-start
  0.6 83.5 %shard_map.76 = (f32[32,40,512]{2,1,0:T(8,128)S(1)}, f32[32,1,640]{2,1,0:T(1,128)S(1)}, f32[3,40,120]{2,1,0:T(8,128)S(1)}) custom-call(f32[120,16384]{1,0:T(8,128)} %u_hbm.1, f32[1,16384]{1,0:T(1,128)} %r_hbm.1, f32[40,120]{1,0:T(8,128)} %bitcast.3, f32[3,30,120]{2,1,0:T(8,128)} %bitcast.2), custom_call_target="tpu_custom_call" | custom-call | tf_op jit(solution)/shard_map/pallas_call | solution.py:382
  84.1 0.0 copy-done
  84.1 2.9 %shard_map.77 = (f32[40,16384]{1,0:T(8,128)}, f32[1,16384]{1,0:T(1,128)}, f32[3,40,120]{2,1,0:T(8,128)}) custom-call(s32[1,32]{1,0:T(1,128)S(1)} %copy-done, f32[32,40,512]{2,1,0:T(8,128)S(1)} %get-tuple-element.6.big, f32[32,1,640]{2,1,0:T(1,128)S(1)} %get-tuple-element.7.small, f32[3,40,120]{2,1,0:T(8,128)S(1)} %get-tuple-element.8.coeff), custom_call_target="tpu_custom_call" | custom-call | tf_op jit(solution)/shard_map/pallas_call | solution.py:453
Async XLA Ops:
  0.6 83.5 %copy-start = (s32[1,32]{1,0:T(1,128)S(1)}, s32[1,32]{1,0:T(1,128)}, u32[]{:S(2)}) copy-start(s32[1,32]{1,0:T(1,128)} %slots.1) | copy-start | bytes 388

commit v3 on v2

--- a/solution.py
+++ b/solution.py
@@ -39,49 +39,72 @@
             lax.dot_general(hi, lo, dims, preferred_element_type=jnp.float32))
 
 
-def factor_panels(sums_ref, restart_ref, work, upper, nrows, panel):
-    keep, k = restart_ref.shape
-    width = sums_ref.shape[1]
-    row = lax.broadcasted_iota(jnp.int32, (width, width), 0)
-    lane = lax.broadcasted_iota(jnp.int32, (width, width), 1)
-    line = lax.broadcasted_iota(jnp.int32, (1, width), 1)
-    work[:, :width] = sums_ref[...] * (1.0 / nrows)
-    work[:, width:] = jnp.where(row == lane, 1.0, 0.0)
-    upper[...] = jnp.zeros_like(upper)
-
-    def step(i, carry):
-        base = i * panel
-        rows = [work[pl.ds(base + a, 1), :] for a in range(panel)]
-        left = work[:, :width]
-        cols = [jnp.sum(jnp.where(lane == base + a, left, 0.0), axis=1, keepdims=True) for a in range(panel)]
-        block = {
-            (a, b): jnp.sum(jnp.where(line == base + b, rows[a][:, :width], 0.0), axis=1, keepdims=True)
-            for a in range(panel) for b in range(a, panel)
-        }
-        for a in range(panel):
-            inverse = 1.0 / block[a, a]
-            for b in range(a + 1, panel):
-                ratio = block[a, b] * inverse
-                rows[b] = rows[b] - ratio * rows[a]
-                cols[b] = cols[b] - ratio * cols[a]
-                for c in range(b, panel):
-                    block[b, c] = block[b, c] - ratio * block[a, c]
-            cols[a] = (cols[a], inverse)
-            upper[pl.ds(base + a, 1), :] = rows[a] * lax.rsqrt(block[a, a])
-        work[...] = work[...] - sum((cols[a][0] * cols[a][1]) * rows[a] for a in range(panel))
+def lane_sum(x, mask):
+    return jnp.broadcast_to(jnp.sum(jnp.where(mask, x, 0.0), axis=1, keepdims=True), x.shape)
+
+
+def eliminate(d, base, lane, sub):
+    n = SUBLANES
+    cols = [lane_sum(d, lane == base + b) for b in range(n)]
+    block = {(a, b): jnp.broadcast_to(cols[b][a : a + 1, :], d.shape) for b in range(n) for a in range(b + 1)}
+    panel = (lane >= base) & (lane < base + n)
+    rows = [jnp.where(panel, jnp.where(lane == base + a, 1.0, 0.0), jnp.broadcast_to(d[a : a + 1, :], d.shape))
+            for a in range(n)]
+    ratio, inverse = {}, []
+    for a in range(n):
+        inverse.append(1.0 / block[a, a])
+        for b in range(a + 1, n):
+            ratio[a, b] = block[a, b] * inverse[a]
+            for c in range(b, n):
+                block[b, c] = block[b, c] - ratio[a, b] * block[a, c]
+            rows[b] = rows[b] - ratio[a, b] * rows[a]
+    back = [None] * n
+    for a in range(n - 1, -1, -1):
+        back[a] = rows[a] * inverse[a]
+        for c in range(a + 1, n):
+            back[a] = back[a] - ratio[a, c] * back[c]
+    packed, pivots = rows[0], block[0, 0]
+    for a in range(1, n):
+        packed = jnp.where(sub == a, rows[a], packed)
+        pivots = jnp.where(sub == a, block[a, a], pivots)
+    own = jnp.zeros_like(d)
+    for b in range(n):
+        col = block[0, b]
+        for a in range(1, b + 1):
+            col = jnp.where(sub == a, block[a, b], col)
+        own = jnp.where((lane == base + b) & (sub <= b), col, own)
+    scale = lax.rsqrt(pivots)
+    left = lane < base + n
+    return panel, back, jnp.where(left, packed, 0.0) * scale, jnp.where(left, own, packed) * scale
+
+
+def factor(sums_ref, nrows, k, work, inverse_ref, upper_ref):
+    width = work.shape[1]
+    lane = lax.broadcasted_iota(jnp.int32, (SUBLANES, width), 1)
+    sub = lax.broadcasted_iota(jnp.int32, (SUBLANES, width), 0)
+    work[...] = sums_ref[...] * (1.0 / nrows)
+
+    def step(first, i, carry):
+        base = i * SUBLANES
+        at = pl.ds(pl.multiple_of(base, SUBLANES), SUBLANES)
+        panel, back, inverse_ref[at, :], upper_ref[at, :] = eliminate(work[at, :], base, lane, sub)
+        for g in range(first, width // SUBLANES):
+            w = work[g * SUBLANES : (g + 1) * SUBLANES, :]
+            rest = jnp.where(panel, 0.0, w)
+            for b in range(SUBLANES):
+                rest = rest - lane_sum(w, lane == base + b) * back[b]
+            work[g * SUBLANES : (g + 1) * SUBLANES, :] = rest
         return carry
 
-    lax.fori_loop(0, k // panel, step, 0)
-    both = jnp.dot(restart_ref[...], upper[:k, :], precision=HIGHEST, preferred_element_type=jnp.float32)
-    half = upper[:, :width].T[k : k + 8, :]
-    proj = jnp.dot(half, upper[:, width:], precision=HIGHEST, preferred_element_type=jnp.float32)
-    raised = both[:, :k]
-    weights = jnp.concatenate([both[:, width:], proj], axis=0)[:, :k]
-    return weights, raised
+    steps = k // SUBLANES
+    mid = (steps + 1) // 2
+    lax.fori_loop(0, mid, functools.partial(step, 1), 0)
+    lax.fori_loop(mid, steps, functools.partial(step, mid + 1), 0)
+    return work[k : k + SUBLANES, :]
 
 
 def restart_kernel(ndev, ns, count, nrows, chunk, raw, u_hbm, r_hbm, restart_hbm, coeff_hbm,
-                   big, small, coeff_out, u_ref, r_ref, restart_ref, coeff_ref, part, gathered, mine_ref, other_ref, red, sums, work, upper, weights_ref,
+                   big, small, coeff_out, u_ref, r_ref, restart_ref, coeff_ref, part, gathered, mine_ref, other_ref, red, sums, work, inverse, upper, weights_ref,
                    send, row_send, turn_send, turn_mid, turn_all, raw_ref, load_sem, own_sem,
                    s1, r1, s2, r2, s3, r3, s4, r4, s5, r5, s6, r6, s7, r7):
     r, s = lax.axis_index("rows"), lax.axis_index("sub")
@@ -225,9 +248,10 @@
 
     for load in load_small:
         load.wait()
-    panel = next(p for p in (4, 2, 1) if k % p == 0)
-    weights, raised = factor_panels(sums, restart_ref, work, upper, nrows, panel)
-    weights_ref[...] = weights
+    last = factor(sums, nrows, k, work, inverse, upper)
+    weights_ref[:keep, :] = jnp.dot(restart_ref[...], inverse[...], precision=HIGHEST,
+                                    preferred_element_type=jnp.float32)[:, :k]
+    weights_ref[keep:, :] = -last[:, :k]
 
     def big_copy(j, slot):
         return remote(send.at[j], big.at[slot], s3.at[j], r3.at[slot], (j // ns, j % ns))
@@ -273,7 +297,7 @@
 
     acc = step(1, jnp.zeros((1, bs), jnp.float32))
 
-    width = turn_send.shape[1]
+    raised = jnp.dot(restart_ref[...], upper[...], precision=HIGHEST, preferred_element_type=jnp.float32)[:, :k]
     turn_send[...] = jnp.zeros_like(turn_send)
     for i in range(deg):
         turned = lax.dot_general(coeff_ref[i], raised, (((1,), (1,)), ((), ())), precision=HIGHEST,
@@ -399,8 +423,9 @@
             pltpu.VMEM((size, LANES), f32),
             pltpu.VMEM((size, LANES), f32),
             pltpu.VMEM((LANES, LANES), f32),
-            pltpu.VMEM((LANES, 2 * LANES), f32),
-            pltpu.VMEM((LANES, 2 * LANES), f32),
+            pltpu.VMEM((LANES, LANES), f32),
+            pltpu.VMEM((k, LANES), f32),
+            pltpu.VMEM((k, LANES), f32),
             pltpu.VMEM((keep + SUBLANES, k), f32),
             pltpu.VMEM((ndev, keep, bs), f32),
             pltpu.VMEM((ndev, 1, bs + LANES), f32),

time: 87.2 us -> 85.1 us (0.976)
  Pallas kernels: 86.4 us -> 84.3 us
    pallas_call x1, Pallas kernels: 83.5 us -> 81.4 us  [restart_call(): pl.pallas_call(functools.partial(restart_kernel, ndev, ns, count, u.shape...]
where the time goes in v3:
time: 85.1 us; the launch traced here: 85 us
  Pallas kernels  84.3 us (99%)
    pallas_call x1, Pallas kernels, restart_call(): pl.pallas_call(functools.partial(restart_kernel, ndev, ns, count, u.shape...  81.4 us
    pallas_call x1, Pallas kernels, place(): pl.pallas_call(functools.partial(place_kernel, ndev, nrows), out_shape=(j...  2.95 us

profile of v3, /device:TPU:0, one launch (start us, length us, event | category | flops | bytes accessed | tf_op | source)
XLA Modules:
  0.0 85.0 jit_solution(932804793589802039)
XLA Ops:
  0.6 0.0 copy-start
  0.6 81.4 %shard_map.76 = (f32[32,40,512]{2,1,0:T(8,128)S(1)}, f32[32,1,640]{2,1,0:T(1,128)S(1)}, f32[3,40,120]{2,1,0:T(8,128)S(1)}) custom-call(f32[120,16384]{1,0:T(8,128)} %u_hbm.1, f32[1,16384]{1,0:T(1,128)} %r_hbm.1, f32[40,120]{1,0:T(8,128)} %bitcast.3, f32[3,30,120]{2,1,0:T(8,128)} %bitcast.2), custom_call_target="tpu_custom_call" | custom-call | tf_op jit(solution)/shard_map/pallas_call | solution.py:406
  82.0 0.0 copy-done
  82.0 2.9 %shard_map.77 = (f32[40,16384]{1,0:T(8,128)}, f32[1,16384]{1,0:T(1,128)}, f32[3,40,120]{2,1,0:T(8,128)}) custom-call(s32[1,32]{1,0:T(1,128)S(1)} %copy-done, f32[32,40,512]{2,1,0:T(8,128)S(1)} %get-tuple-element.6.big, f32[32,1,640]{2,1,0:T(1,128)S(1)} %get-tuple-element.7.small, f32[3,40,120]{2,1,0:T(8,128)S(1)} %get-tuple-element.8.coeff), custom_call_target="tpu_custom_call" | custom-call | tf_op jit(solution)/shard_map/pallas_call | solution.py:478
Async XLA Ops:
  0.6 81.4 %copy-start = (s32[1,32]{1,0:T(1,128)S(1)}, s32[1,32]{1,0:T(1,128)}, u32[]{:S(2)}) copy-start(s32[1,32]{1,0:T(1,128)} %slots.1) | copy-start | bytes 388

commit v4 on v3

--- a/solution.py
+++ b/solution.py
@@ -11,7 +11,8 @@
 AXES = ("rows", "sub")
 LANES = 128
 SUBLANES = 8
-RAW_BLOCKS = 2
+RAW_BLOCKS = (2, 2)
+HELD_FROM = 4
 
 
 def greet_all(me, ndev, ns):
@@ -202,25 +203,35 @@
     def raw_source(q):
         return (r // 2 * 2 + (r + q) % 2 - q // 2 * 2 + nr) % nr
 
-    def raw_copies(q):
+    def raw_copy(q):
         t = raw_peer(q)
-        copies = []
-        for c in range(bs // LANES):
-            cols = pl.ds(pl.multiple_of((t * ns + facing) * bs, LANES) + c * LANES, LANES)
-            copies.append(remote(u_ref.at[:, cols], raw_ref.at[q, :, pl.ds(c * LANES, LANES)],
-                                 s7.at[q, c], r7.at[q, c], (t, facing)))
-        return copies
+        cols = pl.ds(pl.multiple_of((t * ns + facing) * bs, LANES), bs)
+        return remote(u_ref.at[:, cols], raw_ref.at[q], s7.at[q], r7.at[q], (t, facing))
+
+    def for_raw(sender, action):
+        for q in range(raw[0]):
+            if q < raw[1]:
+                action(q)
+            else:
+                @pl.when(sender(q) % 2 == 0)
+                def _():
+                    action(q)
 
     def raw_start():
-        for q in range(raw):
-            for copy in raw_copies(q):
-                copy.start()
-
-    def is_raw(j, peer):
-        hit = j == peer(0) * ns + facing
-        for q in range(1, raw):
-            hit = hit | (j == peer(q) * ns + facing)
+        for_raw(lambda q: r, lambda q: raw_copy(q).start())
+
+    def is_raw(j, peer, sender):
+        hit = j < 0
+        for q in range(raw[0]):
+            one = j == peer(q) * ns + facing
+            hit = hit | (one if q < raw[1] else one & (sender(q) % 2 == 0))
         return inner & hit
+
+    def sent_raw(j):
+        return is_raw(j, raw_peer, lambda q: r)
+
+    def came_raw(j):
+        return is_raw(j, raw_source, raw_source)
 
     @pl.when(inner & jnp.logical_not(owning))
     def _():
@@ -274,7 +285,7 @@
 
     def send_block(j, is_across):
         if is_across:
-            @pl.when(jnp.logical_not(is_raw(j, raw_peer)))
+            @pl.when(jnp.logical_not(sent_raw(j)))
             def _():
                 big_copy(j, me).start()
         else:
@@ -287,13 +298,16 @@
             send_block(j, is_across)
         return acc
 
-    def last_step(acc):
-        for t, is_across in order[:-1]:
-            j = r * ns + t
+    def hold(d, acc):
+        for t, _ in order:
+            j = ((r + d) % nr) * ns + t
             send[j], acc = project(j, acc)
-            send_block(j, is_across)
-        big[me], acc = project(me, acc)
         return acc
+
+    def release(d, carry):
+        for t, is_across in order:
+            send_block(((r + d) % nr) * ns + t, is_across)
+        return carry
 
     acc = step(1, jnp.zeros((1, bs), jnp.float32))
 
@@ -327,8 +341,13 @@
         lax.fori_loop(1, nr, body, 0)
 
     along(lambda t: turn_copy(t, s).start())
-    acc = lax.fori_loop(2, nr, step, acc)
-    acc = last_step(acc)
+    held = min(nr, HELD_FROM)
+    acc = lax.fori_loop(2, held, step, acc)
+    acc = lax.fori_loop(held, nr, hold, acc)
+    for t, _ in order[:-1]:
+        j = r * ns + t
+        send[j], acc = project(j, acc)
+    big[me], acc = project(me, acc)
     partial = jnp.sum(acc, axis=1, keepdims=True)
 
     def mark(j, carry):
@@ -337,15 +356,18 @@
 
     lax.fori_loop(0, ndev, mark, 0)
     others(lambda j: small_copy(j, me).start())
+    lax.fori_loop(held, nr, release, 0)
+    for t, is_across in order[:-1]:
+        send_block(r * ns + t, is_across)
     small[me] = row_send[me]
 
     @pl.when(inner)
     def _():
-        for q in range(raw):
-            for copy in raw_copies(q):
-                copy.wait_recv()
+        def finish(q):
+            raw_copy(q).wait_recv()
             y = jnp.dot(weights_ref[:keep, :], raw_ref[q], precision=HIGHEST, preferred_element_type=jnp.float32)
             big[raw_source(q) * ns + facing] = y
+        for_raw(raw_source, finish)
 
     along(lambda t: turn_copy(t, t).wait_recv())
     plane(lambda p: spread_copy(p, r).start())
@@ -360,14 +382,14 @@
     for i in range(deg):
         coeff_out[i] = turned[i * keep : (i + 1) * keep, :] * scale
 
-    def others_cooked(peer, action):
+    def others_cooked(skip, action):
         def body(j):
-            @pl.when(jnp.logical_not(is_raw(j, peer)))
+            @pl.when(jnp.logical_not(skip(j)))
             def _():
                 action(j)
         others(body)
 
-    others_cooked(raw_source, lambda j: big_copy(j, j).wait_recv())
+    others_cooked(came_raw, lambda j: big_copy(j, j).wait_recv())
     others(lambda j: small_copy(j, j).wait_recv())
     groups_not_mine(lambda g: scatter_copy(g, here).wait_send())
 
@@ -378,11 +400,9 @@
 
     @pl.when(inner)
     def _():
-        for q in range(raw):
-            for copy in raw_copies(q):
-                copy.wait_send()
-
-    others_cooked(raw_peer, lambda j: big_copy(j, me).wait_send())
+        for_raw(lambda q: r, lambda q: raw_copy(q).wait_send())
+
+    others_cooked(sent_raw, lambda j: big_copy(j, me).wait_send())
     others(lambda j: small_copy(j, me).wait_send())
     along(lambda t: turn_copy(t, s).wait_send())
     plane(lambda p: spread_copy(p, r).wait_send())
@@ -432,7 +452,7 @@
             pltpu.VMEM((nr * share, lanes), f32),
             pltpu.VMEM((ns, share, lanes), f32),
             pltpu.VMEM((nr, ns, share, lanes), f32),
-            pltpu.VMEM((RAW_BLOCKS, k, bs), f32),
+            pltpu.VMEM((RAW_BLOCKS[0], k, bs), f32),
             dma((u.shape[1] // chunk + 1,)),
             dma((2,)),
             dma((groups,)), dma((ndev // 2,)),
@@ -441,14 +461,14 @@
             dma((ndev,)), dma((ndev,)),
             dma((ns,)), dma((ns,)),
             dma((nr,)), dma((nr,)),
-            dma((RAW_BLOCKS, bs // LANES)), dma((RAW_BLOCKS, bs // LANES)),
+            dma((RAW_BLOCKS[0],)), dma((RAW_BLOCKS[0],)),
         ],
         compiler_params=pltpu.CompilerParams(
             collective_id=0, has_side_effects=True, vmem_limit_bytes=48 * 1024 * 1024),
     )(*[pltpu.with_memory_space_constraint(a, pltpu.MemorySpace.HBM) for a in (u, r, restart, coeff_t)])
 
 
-def place_kernel(ndev, nrows, slots, big, small, coeff, rows_out, vec_out, coeff_out, out_sem):
+def place_kernel(ndev, nrows, slots, big, small, coeff, rows_out, vec_out, coeff_out, vec, out_sem, side_sem):
     bs = big.shape[2]
 
     def put(d):
@@ -462,13 +482,18 @@
         lax.fori_loop(0, ndev, body, 0)
 
     loop(lambda d: put(d).start())
+    put_coeff = pltpu.make_async_copy(coeff, coeff_out, side_sem.at[0])
+    put_coeff.start()
     total = jnp.sum(small[:, 0, bs : bs + LANES], axis=0, keepdims=True)[:, :1]
     scale = lax.rsqrt(total / nrows + 1e-06)
     for d in range(ndev):
         cols = pl.ds(pl.multiple_of(slots[0, d] * bs, bs), bs)
-        vec_out[:, cols] = small[d, 0:1, :bs] * scale
-    coeff_out[...] = coeff[...]
+        vec[:, cols] = small[d, 0:1, :bs] * scale
+    put_vec = pltpu.make_async_copy(vec, vec_out, side_sem.at[1])
+    put_vec.start()
     loop(lambda d: put(d).wait())
+    put_coeff.wait()
+    put_vec.wait()
 
 
 def place(slot_row, big, small, coeff, nrows):
@@ -483,8 +508,9 @@
             jax.ShapeDtypeStruct(coeff.shape, jnp.float32),
         ),
         in_specs=[pl.BlockSpec(memory_space=pltpu.SMEM), vmem, vmem, vmem],
-        out_specs=(hbm, vmem, vmem),
-        scratch_shapes=[pltpu.SemaphoreType.DMA((ndev,))],
+        out_specs=(hbm, hbm, hbm),
+        scratch_shapes=[pltpu.VMEM((1, ndev * bs), jnp.float32), pltpu.SemaphoreType.DMA((ndev,)),
+                        pltpu.SemaphoreType.DMA((2,))],
         compiler_params=pltpu.CompilerParams(vmem_limit_bytes=32 * 1024 * 1024),
     )(slot_row, big, small, coeff)
 

time: 85.1 us -> 84.5 us (level)
  no operation moved by 1% of the time
where the time goes in v4:
time: 84.5 us; the launch traced here: 84.3 us
  Pallas kernels  83.7 us (99%)
    pallas_call x1, Pallas kernels, restart_call(): pl.pallas_call(functools.partial(restart_kernel, ndev, ns, count, u.shape...  81.3 us
    pallas_call x1, Pallas kernels, place(): pl.pallas_call(functools.partial(place_kernel, ndev, nrows), out_shape=(j...  2.36 us

profile of v4, /device:TPU:0, one launch (start us, length us, event | category | flops | bytes accessed | tf_op | source)
XLA Modules:
  0.0 84.3 jit_solution(17454121985194985631)
XLA Ops:
  0.6 0.0 copy-start
  0.6 81.3 %shard_map.76 = (f32[32,40,512]{2,1,0:T(8,128)S(1)}, f32[32,1,640]{2,1,0:T(1,128)S(1)}, f32[3,40,120]{2,1,0:T(8,128)S(1)}) custom-call(f32[120,16384]{1,0:T(8,128)} %u_hbm.1, f32[1,16384]{1,0:T(1,128)} %r_hbm.1, f32[40,120]{1,0:T(8,128)} %bitcast.3, f32[3,30,120]{2,1,0:T(8,128)} %bitcast.2), custom_call_target="tpu_custom_call" | custom-call | tf_op jit(solution)/shard_map/pallas_call | solution.py:426
  81.9 0.0 copy-done
  82.0 2.4 %shard_map.77 = (f32[40,16384]{1,0:T(8,128)}, f32[1,16384]{1,0:T(1,128)}, f32[3,40,120]{2,1,0:T(8,128)}) custom-call(s32[1,32]{1,0:T(1,128)S(1)} %copy-done, f32[32,40,512]{2,1,0:T(8,128)S(1)} %get-tuple-element.6.big, f32[32,1,640]{2,1,0:T(1,128)S(1)} %get-tuple-element.7.small, f32[3,40,120]{2,1,0:T(8,128)S(1)} %get-tuple-element.8.coeff), custom_call_target="tpu_custom_call" | custom-call | tf_op jit(solution)/shard_map/pallas_call | solution.py:503
Async XLA Ops:
  0.6 81.3 %copy-start = (s32[1,32]{1,0:T(1,128)S(1)}, s32[1,32]{1,0:T(1,128)}, u32[]{:S(2)}) copy-start(s32[1,32]{1,0:T(1,128)} %slots.1) | copy-start | bytes 388

commit v5 on v4

--- a/solution.py
+++ b/solution.py
@@ -11,7 +11,8 @@
 AXES = ("rows", "sub")
 LANES = 128
 SUBLANES = 8
-RAW_BLOCKS = (2, 2)
+RAW_BLOCKS = (3, 2)
+RAW_AFTER = 5
 HELD_FROM = 4
 
 
@@ -139,6 +140,46 @@
         load.start()
     barrier = greet_all(me, ndev, ns)
 
+    half = ns // 2
+    inner = (s == half - 1) | (s == half)
+    facing = ns - 1 - s
+
+    def raw_peer(q):
+        return (r // 2 * 2 + (r + q) % 2 + q // 2 * 2) % nr
+
+    def raw_source(q):
+        return (r // 2 * 2 + (r + q) % 2 - q // 2 * 2 + nr) % nr
+
+    def raw_copy(q):
+        t = raw_peer(q)
+        cols = pl.ds(pl.multiple_of((t * ns + facing) * bs, LANES), bs)
+        return remote(u_hbm.at[:, cols], raw_ref.at[q], s7.at[q], r7.at[q], (t, facing))
+
+    def for_raw(sender, action):
+        for q in range(raw[0]):
+            if q < raw[1]:
+                action(q)
+            else:
+                @pl.when(sender(q) % 2 == 0)
+                def _():
+                    action(q)
+
+    def raw_start():
+        for_raw(lambda q: r, lambda q: raw_copy(q).start())
+
+    def is_raw(j, peer, sender):
+        hit = j < 0
+        for q in range(raw[0]):
+            one = j == peer(q) * ns + facing
+            hit = hit | (one if q < raw[1] else one & (sender(q) % 2 == 0))
+        return inner & hit
+
+    def sent_raw(j):
+        return is_raw(j, raw_peer, lambda q: r)
+
+    def came_raw(j):
+        return is_raw(j, raw_source, raw_source)
+
     load_r.wait()
     main = jnp.zeros((LANES, LANES), jnp.float32)
     cross = jnp.zeros((LANES, LANES), jnp.float32)
@@ -147,10 +188,15 @@
         one, two = gram_piece(u_ref, r_ref, c * chunk, chunk)
         main = main + one
         cross = cross + two
+        if c == min(RAW_AFTER, pieces - 1):
+            pl.semaphore_wait(barrier, ndev - 1)
+
+            @pl.when(inner & (r % 2 == 0))
+            def _():
+                raw_start()
+
     part[...] = main + (cross + cross.T)
-    pl.semaphore_wait(barrier, ndev - 1)
-
-    half = ns // 2
+
     side, pos = s // half, s % half
     here = r * half + pos
     size = red.shape[0]
@@ -194,46 +240,7 @@
 
     groups_not_mine(lambda g: scatter_copy(g, here).start())
 
-    inner = (s == half - 1) | (s == half)
-    facing = ns - 1 - s
-
-    def raw_peer(q):
-        return (r // 2 * 2 + (r + q) % 2 + q // 2 * 2) % nr
-
-    def raw_source(q):
-        return (r // 2 * 2 + (r + q) % 2 - q // 2 * 2 + nr) % nr
-
-    def raw_copy(q):
-        t = raw_peer(q)
-        cols = pl.ds(pl.multiple_of((t * ns + facing) * bs, LANES), bs)
-        return remote(u_ref.at[:, cols], raw_ref.at[q], s7.at[q], r7.at[q], (t, facing))
-
-    def for_raw(sender, action):
-        for q in range(raw[0]):
-            if q < raw[1]:
-                action(q)
-            else:
-                @pl.when(sender(q) % 2 == 0)
-                def _():
-                    action(q)
-
-    def raw_start():
-        for_raw(lambda q: r, lambda q: raw_copy(q).start())
-
-    def is_raw(j, peer, sender):
-        hit = j < 0
-        for q in range(raw[0]):
-            one = j == peer(q) * ns + facing
-            hit = hit | (one if q < raw[1] else one & (sender(q) % 2 == 0))
-        return inner & hit
-
-    def sent_raw(j):
-        return is_raw(j, raw_peer, lambda q: r)
-
-    def came_raw(j):
-        return is_raw(j, raw_source, raw_source)
-
-    @pl.when(inner & jnp.logical_not(owning))
+    @pl.when(inner & (r % 2 == 1) & jnp.logical_not(owning))
     def _():
         raw_start()
 
@@ -245,15 +252,16 @@
         total = jnp.sum(gathered[...], axis=0)
         mine_ref[...] = total
         cross_copy().start()
+
+        @pl.when(inner)
+        def _():
+            raw_start()
+
         cross_copy().wait_recv()
         total = total + other_ref[...]
         red[...] = total
         sums[mine, :] = total
         half_others(lambda m: gather_copy(m, own).start())
-
-    @pl.when(inner & owning)
-    def _():
-        raw_start()
 
     groups_not_mine(lambda g: gather_copy(here, g).wait_recv())
 

time: 84.5 us -> 84 us (level)
  Pallas kernels: 83.7 us -> 82.8 us
where the time goes in v5:
time: 84 us; the launch traced here: 83.5 us
  Pallas kernels  82.8 us (99%)
    pallas_call x1, Pallas kernels, restart_call(): pl.pallas_call(functools.partial(restart_kernel, ndev, ns, count, u.shape...  80.5 us
    pallas_call x1, Pallas kernels, place(): pl.pallas_call(functools.partial(place_kernel, ndev, nrows), out_shape=(j...  2.36 us

profile of v5, /device:TPU:0, one launch (start us, length us, event | category | flops | bytes accessed | tf_op | source)
XLA Modules:
  0.0 83.5 jit_solution(8374140515155213756)
XLA Ops:
  0.6 0.0 copy-start
  0.6 80.5 %shard_map.76 = (f32[32,40,512]{2,1,0:T(8,128)S(1)}, f32[32,1,640]{2,1,0:T(1,128)S(1)}, f32[3,40,120]{2,1,0:T(8,128)S(1)}) custom-call(f32[120,16384]{1,0:T(8,128)} %u_hbm.1, f32[1,16384]{1,0:T(1,128)} %r_hbm.1, f32[40,120]{1,0:T(8,128)} %bitcast.3, f32[3,30,120]{2,1,0:T(8,128)} %bitcast.2), custom_call_target="tpu_custom_call" | custom-call | tf_op jit(solution)/shard_map/pallas_call | solution.py:434
  81.1 0.0 copy-done
  81.1 2.4 %shard_map.77 = (f32[40,16384]{1,0:T(8,128)}, f32[1,16384]{1,0:T(1,128)}, f32[3,40,120]{2,1,0:T(8,128)}) custom-call(s32[1,32]{1,0:T(1,128)S(1)} %copy-done, f32[32,40,512]{2,1,0:T(8,128)S(1)} %get-tuple-element.6.big, f32[32,1,640]{2,1,0:T(1,128)S(1)} %get-tuple-element.7.small, f32[3,40,120]{2,1,0:T(8,128)S(1)} %get-tuple-element.8.coeff), custom_call_target="tpu_custom_call" | custom-call | tf_op jit(solution)/shard_map/pallas_call | solution.py:511
Async XLA Ops:
  0.6 80.5 %copy-start = (s32[1,32]{1,0:T(1,128)S(1)}, s32[1,32]{1,0:T(1,128)}, u32[]{:S(2)}) copy-start(s32[1,32]{1,0:T(1,128)} %slots.1) | copy-start | bytes 388

commit v6 on v5

--- a/solution.py
+++ b/solution.py
@@ -38,7 +38,7 @@
     lo = (x - hi.astype(jnp.float32)).astype(jnp.bfloat16)
     dims = (((1,), (1,)), ((), ()))
     return (lax.dot_general(hi, hi, dims, preferred_element_type=jnp.float32),
-            lax.dot_general(hi, lo, dims, preferred_element_type=jnp.float32))
+            lax.dot_general(lo, hi, dims, preferred_element_type=jnp.float32))
 
 
 def lane_sum(x, mask):
@@ -145,10 +145,11 @@
     facing = ns - 1 - s
 
     def raw_peer(q):
-        return (r // 2 * 2 + (r + q) % 2 + q // 2 * 2) % nr
+        pair = r // 2
+        return (pair // 2 * 2 + (pair + q // 2) % 2) * 2 + (r + q) % 2
 
     def raw_source(q):
-        return (r // 2 * 2 + (r + q) % 2 - q // 2 * 2 + nr) % nr
+        return raw_peer(q)
 
     def raw_copy(q):
         t = raw_peer(q)
@@ -233,10 +234,8 @@
         lax.fori_loop(0, groups, body, 0)
 
     def half_others(action):
-        def body(o, carry):
+        for o in range(1, nr * half):
             action((here + o) % (nr * half))
-            return carry
-        lax.fori_loop(1, nr * half, body, 0)
 
     groups_not_mine(lambda g: scatter_copy(g, here).start())
 

time: 84 us -> 83.6 us (level)
  no operation moved by 1% of the time
where the time goes in v6:
time: 83.6 us; the launch traced here: 83.3 us
  Pallas kernels  82.6 us (99%)
    pallas_call x1, Pallas kernels, restart_call(): pl.pallas_call(functools.partial(restart_kernel, ndev, ns, count, u.shape...  80.2 us
    pallas_call x1, Pallas kernels, place(): pl.pallas_call(functools.partial(place_kernel, ndev, nrows), out_shape=(j...  2.36 us

profile of v6, /device:TPU:0, one launch (start us, length us, event | category | flops | bytes accessed | tf_op | source)
XLA Modules:
  0.0 83.3 jit_solution(14529920300056427678)
XLA Ops:
  0.6 0.0 copy-start
  0.6 80.2 %shard_map.76 = (f32[32,40,512]{2,1,0:T(8,128)S(1)}, f32[32,1,640]{2,1,0:T(1,128)S(1)}, f32[3,40,120]{2,1,0:T(8,128)S(1)}) custom-call(f32[120,16384]{1,0:T(8,128)} %u_hbm.1, f32[1,16384]{1,0:T(1,128)} %r_hbm.1, f32[40,120]{1,0:T(8,128)} %bitcast.3, f32[3,30,120]{2,1,0:T(8,128)} %bitcast.2), custom_call_target="tpu_custom_call" | custom-call | tf_op jit(solution)/shard_map/pallas_call | solution.py:433
  80.9 0.0 copy-done
  80.9 2.4 %shard_map.77 = (f32[40,16384]{1,0:T(8,128)}, f32[1,16384]{1,0:T(1,128)}, f32[3,40,120]{2,1,0:T(8,128)}) custom-call(s32[1,32]{1,0:T(1,128)S(1)} %copy-done, f32[32,40,512]{2,1,0:T(8,128)S(1)} %get-tuple-element.6.big, f32[32,1,640]{2,1,0:T(1,128)S(1)} %get-tuple-element.7.small, f32[3,40,120]{2,1,0:T(8,128)S(1)} %get-tuple-element.8.coeff), custom_call_target="tpu_custom_call" | custom-call | tf_op jit(solution)/shard_map/pallas_call | solution.py:510
Async XLA Ops:
  0.6 80.3 %copy-start = (s32[1,32]{1,0:T(1,128)S(1)}, s32[1,32]{1,0:T(1,128)}, u32[]{:S(2)}) copy-start(s32[1,32]{1,0:T(1,128)} %slots.1) | copy-start | bytes 388
